TPU v7x, 32 devices: a whole 2x2x4 slice. The times are simulated.
32 devices in a mesh: client: 8 (over z, x), head: 4 (over y, core).
Axes of the slice: x: 2, y: 2, z: 4, core: 2. Of those that a mesh axis runs over, the one named last changes fastest.
Arguments:
- pre: bfloat16 [10240, 4096], P('client'), may hold values from -40 to 40
- delta: float32 [10240, 4096], P('client', 'head'), may hold values from -300 to 300
- head_weight: bfloat16 [4096, 4096], P(None, 'head'), may hold values from -0.09375 to 0.09375
- client_ids: int32 [128], P('client'), may hold values from 0 to 127, as said below
Outputs:
- head_grad: float32 [4096, 4096], P('client', 'head')
- bias_grad: float32 [4096], P('head')
- embed_grad: float32 [128, 4096], P('client', 'head')
- span_grad: float32 [80, 4096], P(None, 'head')
Inputs may be any that keep to these rules, and one draw needn't show every extreme that they name: `client_ids`: each of the 128 clients appears exactly once.
All inputs are finite; a program needn't handle non-finite values.
Results may differ from a plain program's by a relative error of at most 0.024.
Values may be sent and summed in bfloat16 or wider, within the bound.
A program may use at most 128 MiB of HBM per device.

v0:
```python
import jax
import jax.numpy as jnp
from jax import lax
from jax.sharding import PartitionSpec as P

EPSILON = 1e-06


def silu_slope(values):
    sigma = jax.nn.sigmoid(values)
    return sigma * (1.0 + values * (1.0 - sigma))


def clip_factor(total, number):
    return jnp.minimum(1.0, 1.0 / jnp.sqrt(total / number + EPSILON))


def per_device(pre, delta, head_weight, client_ids):
    rows_here, hidden_width = pre.shape
    emit_here = delta.shape[1]
    clients_here = client_ids.shape[0]
    span_count = rows_here // clients_here
    head_devices = lax.axis_size("head")
    client_devices = lax.axis_size("client")
    hidden = jax.nn.silu(pre.astype(jnp.float32)).astype(jnp.bfloat16)
    delta_low = delta.astype(jnp.bfloat16)
    head_raw = lax.psum_scatter(
        lax.dot_general(
            hidden, delta_low, (((0,), (0,)), ((), ())), preferred_element_type=jnp.float32
        ).astype(jnp.bfloat16),
        "client",
        scatter_dimension=0,
        tiled=True,
    ).astype(jnp.float32)
    head_square = jnp.sum(head_raw * head_raw)
    head_square = lax.psum(head_square, ("client", "head"))
    bias_local = jnp.sum(delta, axis=0)
    partial_sum = lax.dot_general(
        delta_low, head_weight, (((1,), (1,)), ((), ())), preferred_element_type=jnp.float32
    )
    rounded = lax.optimization_barrier(partial_sum.astype(jnp.bfloat16))
    block_grad = rounded.astype(jnp.float32) * silu_slope(pre.astype(jnp.float32))
    grouped = block_grad.reshape(clients_here, span_count, hidden_width)
    client_whole = jnp.sum(grouped, axis=1)
    span_whole = jnp.sum(grouped, axis=0)
    client_part, span_part = (
        lax.psum_scatter(
            client_whole.astype(jnp.bfloat16), "head", scatter_dimension=1, tiled=True
        ).astype(jnp.float32),
        lax.psum_scatter(
            span_whole.astype(jnp.bfloat16), "head", scatter_dimension=1, tiled=True
        ).astype(jnp.float32),
    )
    span_raw, bias_raw = (
        lax.psum(span_part.astype(jnp.bfloat16), "client").astype(jnp.float32),
        lax.psum(bias_local.astype(jnp.bfloat16), "client").astype(jnp.float32),
    )
    targets = lax.iota(jnp.int32, lax.axis_size("client") * clients_here)
    selector = (targets[:, None] == client_ids[None, :]).astype(jnp.float32)
    embed_raw = lax.psum_scatter(
        jnp.dot(
            selector,
            client_part,
            precision=lax.Precision.HIGHEST,
            preferred_element_type=jnp.float32,
        ).astype(jnp.bfloat16),
        "client",
        scatter_dimension=0,
        tiled=True,
    ).astype(jnp.float32)
    leading = (lax.axis_index("client") == 0).astype(jnp.float32)
    small_square = leading * (jnp.sum(span_raw * span_raw) + jnp.sum(bias_raw * bias_raw))
    embed_square = jnp.sum(embed_raw * embed_raw)
    embed_total, small_total = lax.psum((embed_square, small_square), ("client", "head"))
    emit_total = emit_here * head_devices
    clients_total = clients_here * client_devices
    head_factor = clip_factor(head_square, hidden_width * emit_total)
    embed_factor = clip_factor(embed_total, clients_total * hidden_width)
    rest_factor = clip_factor(small_total, span_count * hidden_width + emit_total)
    return (
        head_factor * head_raw,
        rest_factor * bias_raw,
        embed_factor * embed_raw,
        rest_factor * span_raw,
    )


def solution(mesh):
    placed = (P("client", None), P("client", "head"), P(None, "head"), P("client"))
    return jax.shard_map(
        per_device,
        mesh=mesh,
        in_specs=placed,
        out_specs=(P("client", "head"), P("head"), P("client", "head"), P(None, "head")),
        check_vma=False,
    )
```

profile of v0, /device:TPU:0, one launch (start us, length us, event | category | flops | bytes accessed | tf_op | source)
XLA Modules:
  0.0 433.6 jit_solution(12990887152646815512)
XLA Ops:
  7.2 17.6 %convolution_convert_fusion = bf16[1280,4096]{1,0:T(8,128)(2,1)} fusion(bf16[4096,1024]{1,0:T(8,128)(2,1)} %param.6, f32[1280,1024]{1,0:T(8,128)} %param.5), kind=kOutput, calls=%fused_computation.10 | convolution fusion | flops 10743971840 | bytes 24117248 | tf_op jit(solution)/shard_map/dot_general | solution.py:38
  24.8 9.6 %fusion.6 = f32[1280,4096]{1,0:T(8,128)S(1)} fusion(bf16[1280,4096]{1,0:T(8,128)(2,1)S(1)} %copy-done, bf16[1280,4096]{1,0:T(8,128)(2,1)} %convolution_convert_fusion), kind=kLoop, calls=%fused_computation.9 | loop fusion | flops 52428800 | bytes 41943040 | tf_op jit(solution)/shard_map/mul | solution.py:42
  34.4 5.2 %fusion.20 = (bf16[16,4096]{1,0:T(8,128)(2,1)}, bf16[80,4096]{1,0:T(8,128)(2,1)}) fusion(f32[16,80,4096]{2,1,0:T(8,128)S(1)} %bitcast.3), kind=kLoop, calls=%fused_computation.31 | loop fusion | flops 10092544 | bytes 21757952 | tf_op jit(solution)/shard_map/reduce_sum | solution.py:44
  39.6 0.0 reduce-scatter.7.cloned.1.call-start
  39.6 0.7 reduce-scatter.7.cloned.1.call-update
  40.4 21.7 %reduce-scatter.9.cloned.1.call-done = bf16[16,1024]{1,0:T(8,128)(2,1)} async-done(((bf16[16,4096]{1,0:T(8,128)(2,1)}), bf16[16,1024]{1,0:T(8,128)(2,1)}) %reduce-scatter.9.cloned.1.call-update) | async-done | bytes 32784 | tf_op jit(solution)/shard_map/reduce_scatter | solution.py:47
  62.1 1.7 convolution_convert_fusion.1
  63.8 23.8 %reduce-scatter.7.cloned.1.call-done = bf16[80,1024]{1,0:T(8,128)(2,1)} async-done(((bf16[80,4096]{1,0:T(8,128)(2,1)}), bf16[80,1024]{1,0:T(8,128)(2,1)}) %reduce-scatter.7.cloned.1.call-update) | async-done | bytes 163856 | tf_op jit(solution)/shard_map/reduce_scatter | solution.py:50
  87.6 0.2 reduce-scatter.5.cloned.1.call-start
  87.9 18.3 %fusion.9 = bf16[4096,1024]{1,0:T(8,128)(2,1)} fusion(bf16[1280,4096]{1,0:T(8,128)(2,1)} %param.4, f32[1280,1024]{1,0:T(8,128)} %param.5), kind=kOutput, calls=%fused_computation.12 | convolution fusion | flops 10774380544 | bytes 24117248 | tf_op jit(solution)/shard_map/dot_general | solution.py:28
  106.2 2.9 reduce_sum.66
  109.0 21.5 %psum.37 = bf16[1024]{0:T(1024)(128)(2,1)S(1)} all-reduce(bf16[1024]{0:T(1024)(128)(2,1)S(1)} %reduce_sum.66), channel_id=1, replica_groups=mesh['client'=8,'head'=4] {'client'}, use_global_device_ids=true, to_apply=%region_8.9 | all-reduce | flops 1024 | bytes 4096 | tf_op jit(solution)/shard_map/psum | solution.py:56
  130.5 0.6 fusion.18
  131.1 22.5 %reduce-scatter.11.cloned.1.call-done = bf16[16,1024]{1,0:T(8,128)(2,1)} async-done(((bf16[128,1024]{1,0:T(8,128)(2,1)}), bf16[16,1024]{1,0:T(8,128)(2,1)}) %reduce-scatter.11.cloned.1.call-update) | async-done | bytes 32784 | tf_op jit(solution)/shard_map/reduce_scatter | solution.py:60
  153.6 1.4 fusion.16
  155.0 70.9 %all-reduce.3.cloned.1.call-done = bf16[80,1024]{1,0:T(8,128)(2,1)} async-done(((bf16[80,1024]{1,0:T(8,128)(2,1)}), bf16[80,1024]{1,0:T(8,128)(2,1)}) %all-reduce.3.cloned.1.call-update) | async-done | bytes 163856 | tf_op jit(solution)/shard_map/psum | solution.py:55
  225.9 1.6 fusion.15
  228.8 147.9 %reduce-scatter.5.cloned.1.call-done = bf16[512,1024]{1,0:T(8,128)(2,1)} async-done(((bf16[4096,1024]{1,0:T(8,128)(2,1)}), bf16[512,1024]{1,0:T(8,128)(2,1)}) %reduce-scatter.5.cloned.1.call-update) | async-done | bytes 1048592 | tf_op jit(solution)/shard_map/reduce_scatter | solution.py:27
  376.7 2.4 fusion.12
  379.0 39.5 %all-reduce = (f32[]{:T(128)}, f32[]{:T(128)}, f32[]{:T(128)}) all-reduce(f32[]{:T(128)} %fusion.12, f32[]{:T(128)S(6)} %mul.61, f32[]{:T(128)} %fusion.16), channel_id=1, replica_groups=mesh['client'=8,'head'=4] {'client','head'}, use_global_device_ids=true, to_apply=%region_2.3 | all-reduce | flops 3 | bytes 24 | tf_op jit(solution)/shard_map/psum | solution.py:36
  419.9 0.6 convert_multiply_fusion.8
  421.2 1.7 convert_multiply_fusion.4
  422.9 1.4 convert_multiply_fusion.6
  424.3 2.8 convert_multiply_fusion.2
  (11 shorter events, 0.2 us)
Async XLA Ops:
  7.2 54.9 %reduce-scatter.9.cloned.1.call-start = ((), (), s32[]{:S(2)}) async-start(), calls=%async_computation.7 | async-start | bytes 163840 | tf_op jit(solution)/shard_map/reduce_scatter | solution.py:47
  7.2 17.6 %copy-start = (bf16[1280,4096]{1,0:T(8,128)(2,1)S(1)}, bf16[1280,4096]{1,0:T(8,128)(2,1)}, u32[]{:S(2)}) copy-start(bf16[1280,4096]{1,0:T(8,128)(2,1)} %param.4) | copy-start | bytes 31457284
  34.4 27.7 %copy-start.1 = (s32[16]{0:T(128)S(1)}, s32[16]{0:T(128)}, u32[]{:S(2)}) copy-start(s32[16]{0:T(128)} %param.7) | copy-start | bytes 196
  39.6 48.0 %reduce-scatter.7.cloned.1.call-start = ((), (), s32[]{:S(2)}) async-start(), calls=%async_computation.5 | async-start | bytes 819200 | tf_op jit(solution)/shard_map/reduce_scatter | solution.py:50
  40.3 113.3 %reduce-scatter.11.cloned.1.call-start = ((), (), s32[]{:S(2)}) async-start(), calls=%async_computation.8 | async-start | bytes 294912 | tf_op jit(solution)/shard_map/reduce_scatter | solution.py:60
  63.8 162.1 %all-reduce.3.cloned.1.call-start = ((), (), s32[]{:S(2)}) async-start(), calls=%async_computation.6 | async-start | bytes 327680 | tf_op jit(solution)/shard_map/psum | solution.py:55
  87.6 289.0 %reduce-scatter.5.cloned.1.call-start = ((), (), s32[]{:S(2)}) async-start(), calls=%async_computation.4 | async-start | bytes 9437184 | tf_op jit(solution)/shard_map/reduce_scatter | solution.py:27
Sparse Core Ops, SparseCore 0:
  39.7 22.3 reduce-scatter.8
  65.1 22.4 reduce-scatter.6
  91.5 62.0 reduce-scatter.10
  156.8 69.0 all-reduce.2
  229.3 147.2 reduce-scatter.4
where the time goes:
time: 434 us
  waiting for transfers between devices  288 us (66%)
  blocking collectives  61 us (14%)
  matrix products  37.5 us (9%)
  other arithmetic  30 us (7%)
  between operations  17.2 us (4%)
    reduce_scatter x1, waiting for transfers between devices, per_device(): lax.psum_scatter(lax.dot_general(hidden, delta_low, (((0,), (0,)), ((), (...  148 us
    psum x1, waiting for transfers between devices, per_device(): lax.psum(span_part.astype(jnp.bfloat16), 'client').astype(jnp.float32)  70.9 us
    psum x1, blocking collectives, per_device(): head_square = lax.psum(head_square, ('client', 'head'))  39.5 us
    reduce_scatter x1, waiting for transfers between devices, per_device(): lax.psum_scatter(span_whole.astype(jnp.bfloat16), 'head', scatter_dimensi...  23.8 us
    reduce_scatter x1, waiting for transfers between devices, per_device(): lax.psum_scatter(jnp.dot(selector, client_part, precision=lax.Precision.H...  22.5 us
    reduce_scatter x1, waiting for transfers between devices, per_device(): lax.psum_scatter(client_whole.astype(jnp.bfloat16), 'head', scatter_dimen...  21.7 us
    psum x1, blocking collectives, per_device(): lax.psum(bias_local.astype(jnp.bfloat16), 'client').astype(jnp.float32)  21.5 us
    dot_general x1, matrix products, per_device(): lax.dot_general(hidden, delta_low, (((0,), (0,)), ((), ())), preferred_el...  18.3 us
  transfers between devices with their start and end apart: 5, of which 5 were waited for; matrix products, arithmetic and copies ran while one was open for 6% of the time, Pallas kernels for 0%

commit v1 on v0

--- a/solution.py
+++ b/solution.py
@@ -33,7 +33,7 @@
         tiled=True,
     ).astype(jnp.float32)
     head_square = jnp.sum(head_raw * head_raw)
-    head_square = lax.psum(head_square, ("client", "head"))
+    head_square = lax.psum(lax.psum(head_square, "head"), "client")
     bias_local = jnp.sum(delta, axis=0)
     partial_sum = lax.dot_general(
         delta_low, head_weight, (((1,), (1,)), ((), ())), preferred_element_type=jnp.float32

time: 434 us -> 420 us (0.968)
  waiting for transfers between devices: 288 us -> 241 us
  blocking collectives: 61 us -> 93.3 us
    reduce_scatter x1, waiting for transfers between devices: 148 us -> 102 us  [per_device(): lax.psum_scatter(lax.dot_general(hidden, delta_low, (((0,), (0,)), ((), (...]
    psum x1 -> x3, blocking collectives: 39.5 us -> 71.8 us  [the longest x1 44.3 us: per_device(): lax.psum((embed_square, small_square), ('client', 'head'))]
  transfers between devices with their start and end apart: 5 -> 5, of which waited for: 5 -> 5; matrix products, arithmetic and copies ran while one was open for 6% -> 7% of each run, Pallas kernels for 0% -> 0%
where the time goes in v1:
time: 420 us
  waiting for transfers between devices  241 us (57%)
  blocking collectives  93.3 us (22%)
  matrix products  37.5 us (9%)
  other arithmetic  30 us (7%)
  between operations  17.2 us (4%)
    reduce_scatter x1, waiting for transfers between devices, per_device(): lax.psum_scatter(lax.dot_general(hidden, delta_low, (((0,), (0,)), ((), (...  102 us
    psum x1, waiting for transfers between devices, per_device(): lax.psum(span_part.astype(jnp.bfloat16), 'client').astype(jnp.float32)  70.9 us
    psum x1, blocking collectives, per_device(): lax.psum((embed_square, small_square), ('client', 'head'))  44.3 us
    psum x2, blocking collectives, per_device(): head_square = lax.psum(lax.psum(head_square, 'head'), 'client')  27.5 us
    reduce_scatter x1, waiting for transfers between devices, per_device(): lax.psum_scatter(span_whole.astype(jnp.bfloat16), 'head', scatter_dimensi...  23.8 us
    reduce_scatter x1, waiting for transfers between devices, per_device(): lax.psum_scatter(jnp.dot(selector, client_part, precision=lax.Precision.H...  22.5 us
    reduce_scatter x1, waiting for transfers between devices, per_device(): lax.psum_scatter(client_whole.astype(jnp.bfloat16), 'head', scatter_dimen...  21.7 us
    psum x1, blocking collectives, per_device(): lax.psum(bias_local.astype(jnp.bfloat16), 'client').astype(jnp.float32)  21.5 us
  transfers between devices with their start and end apart: 5, of which 5 were waited for; matrix products, arithmetic and copies ran while one was open for 7% of the time, Pallas kernels for 0%

profile of v1, /device:TPU:0, one launch (start us, length us, event | category | flops | bytes accessed | tf_op | source)
XLA Modules:
  0.0 419.7 jit_solution(8034545761507809878)
XLA Ops:
  7.2 17.6 %convolution_convert_fusion = bf16[1280,4096]{1,0:T(8,128)(2,1)} fusion(bf16[4096,1024]{1,0:T(8,128)(2,1)} %param.6, f32[1280,1024]{1,0:T(8,128)} %param.5), kind=kOutput, calls=%fused_computation.10 | convolution fusion | flops 10743971840 | bytes 24117248 | tf_op jit(solution)/shard_map/dot_general | solution.py:38
  24.8 9.6 %fusion.6 = f32[1280,4096]{1,0:T(8,128)S(1)} fusion(bf16[1280,4096]{1,0:T(8,128)(2,1)S(1)} %copy-done, bf16[1280,4096]{1,0:T(8,128)(2,1)} %convolution_convert_fusion), kind=kLoop, calls=%fused_computation.9 | loop fusion | flops 52428800 | bytes 41943040 | tf_op jit(solution)/shard_map/mul | solution.py:42
  34.4 5.2 %fusion.20 = (bf16[16,4096]{1,0:T(8,128)(2,1)}, bf16[80,4096]{1,0:T(8,128)(2,1)}) fusion(f32[16,80,4096]{2,1,0:T(8,128)S(1)} %bitcast.3), kind=kLoop, calls=%fused_computation.31 | loop fusion | flops 10092544 | bytes 21757952 | tf_op jit(solution)/shard_map/reduce_sum | solution.py:44
  39.6 0.7 reduce-scatter.7.cloned.1.call-update
  40.4 21.7 %reduce-scatter.9.cloned.1.call-done = bf16[16,1024]{1,0:T(8,128)(2,1)} async-done(((bf16[16,4096]{1,0:T(8,128)(2,1)}), bf16[16,1024]{1,0:T(8,128)(2,1)}) %reduce-scatter.9.cloned.1.call-update) | async-done | bytes 32784 | tf_op jit(solution)/shard_map/reduce_scatter | solution.py:47
  62.1 1.7 convolution_convert_fusion.1
  63.8 23.8 %reduce-scatter.7.cloned.1.call-done = bf16[80,1024]{1,0:T(8,128)(2,1)} async-done(((bf16[80,4096]{1,0:T(8,128)(2,1)}), bf16[80,1024]{1,0:T(8,128)(2,1)}) %reduce-scatter.7.cloned.1.call-update) | async-done | bytes 163856 | tf_op jit(solution)/shard_map/reduce_scatter | solution.py:50
  87.9 18.3 %fusion.9 = bf16[4096,1024]{1,0:T(8,128)(2,1)} fusion(bf16[1280,4096]{1,0:T(8,128)(2,1)} %param.4, f32[1280,1024]{1,0:T(8,128)} %param.5), kind=kOutput, calls=%fused_computation.12 | convolution fusion | flops 10774380544 | bytes 24117248 | tf_op jit(solution)/shard_map/dot_general | solution.py:28
  106.2 2.9 reduce_sum.66
  109.0 21.5 %psum.45 = bf16[1024]{0:T(1024)(128)(2,1)S(1)} all-reduce(bf16[1024]{0:T(1024)(128)(2,1)S(1)} %reduce_sum.66), channel_id=1, replica_groups=mesh['client'=8,'head'=4] {'client'}, use_global_device_ids=true, to_apply=%region_9.10 | all-reduce | flops 1024 | bytes 4096 | tf_op jit(solution)/shard_map/psum | solution.py:56
  130.5 0.6 fusion.18
  131.1 22.5 %reduce-scatter.11.cloned.1.call-done = bf16[16,1024]{1,0:T(8,128)(2,1)} async-done(((bf16[128,1024]{1,0:T(8,128)(2,1)}), bf16[16,1024]{1,0:T(8,128)(2,1)}) %reduce-scatter.11.cloned.1.call-update) | async-done | bytes 32784 | tf_op jit(solution)/shard_map/reduce_scatter | solution.py:60
  153.6 1.4 fusion.16
  155.0 70.9 %all-reduce.3.cloned.1.call-done = bf16[80,1024]{1,0:T(8,128)(2,1)} async-done(((bf16[80,1024]{1,0:T(8,128)(2,1)}), bf16[80,1024]{1,0:T(8,128)(2,1)}) %all-reduce.3.cloned.1.call-update) | async-done | bytes 163856 | tf_op jit(solution)/shard_map/psum | solution.py:55
  225.9 1.6 fusion.15
  228.8 44.3 %all-reduce = (f32[]{:T(128)}, f32[]{:T(128)}) all-reduce(f32[]{:T(128)S(6)} %mul.61, f32[]{:T(128)} %fusion.16), channel_id=1, replica_groups=mesh['client'=8,'head'=4] {'client','head'}, use_global_device_ids=true, to_apply=%region_11.12 | all-reduce | flops 2 | bytes 16 | tf_op jit(solution)/shard_map/psum | solution.py:74
  274.5 1.7 convert_multiply_fusion.4
  276.1 101.6 %reduce-scatter.5.cloned.1.call-done = bf16[512,1024]{1,0:T(8,128)(2,1)} async-done(((bf16[4096,1024]{1,0:T(8,128)(2,1)}), bf16[512,1024]{1,0:T(8,128)(2,1)}) %reduce-scatter.5.cloned.1.call-update) | async-done | bytes 1048592 | tf_op jit(solution)/shard_map/reduce_scatter | solution.py:27
  377.7 2.4 fusion.12
  380.1 1.4 convert_multiply_fusion.6
  381.5 6.9 %psum.42 = f32[]{:T(128)} all-reduce(f32[]{:T(128)} %fusion.12), channel_id=1, replica_groups=mesh['client'=8,'head'=4] {'head'}, use_global_device_ids=true, to_apply=%region_2.3 | all-reduce | flops 1 | bytes 8 | tf_op jit(solution)/shard_map/psum | solution.py:36
  388.3 0.6 convert_multiply_fusion.8
  388.9 20.7 %psum.43 = f32[]{:T(128)} all-reduce(f32[]{:T(128)} %psum.42), channel_id=1, replica_groups=mesh['client'=8,'head'=4] {'client'}, use_global_device_ids=true, to_apply=%region_3.4 | all-reduce | flops 1 | bytes 8 | tf_op jit(solution)/shard_map/psum | solution.py:36
  410.3 2.8 convert_multiply_fusion.2
  (13 shorter events, 0.5 us)
Async XLA Ops:
  7.2 54.9 %reduce-scatter.9.cloned.1.call-start = ((), (), s32[]{:S(2)}) async-start(), calls=%async_computation.7 | async-start | bytes 163840 | tf_op jit(solution)/shard_map/reduce_scatter | solution.py:47
  7.2 17.6 %copy-start = (bf16[1280,4096]{1,0:T(8,128)(2,1)S(1)}, bf16[1280,4096]{1,0:T(8,128)(2,1)}, u32[]{:S(2)}) copy-start(bf16[1280,4096]{1,0:T(8,128)(2,1)} %param.4) | copy-start | bytes 31457284
  34.4 27.7 %copy-start.1 = (s32[16]{0:T(128)S(1)}, s32[16]{0:T(128)}, u32[]{:S(2)}) copy-start(s32[16]{0:T(128)} %param.7) | copy-start | bytes 196
  39.6 48.0 %reduce-scatter.7.cloned.1.call-start = ((), (), s32[]{:S(2)}) async-start(), calls=%async_computation.5 | async-start | bytes 819200 | tf_op jit(solution)/shard_map/reduce_scatter | solution.py:50
  40.3 113.3 %reduce-scatter.11.cloned.1.call-start = ((), (), s32[]{:S(2)}) async-start(), calls=%async_computation.8 | async-start | bytes 294912 | tf_op jit(solution)/shard_map/reduce_scatter | solution.py:60
  63.8 162.1 %all-reduce.3.cloned.1.call-start = ((), (), s32[]{:S(2)}) async-start(), calls=%async_computation.6 | async-start | bytes 327680 | tf_op jit(solution)/shard_map/psum | solution.py:55
  87.6 290.1 %reduce-scatter.5.cloned.1.call-start = ((), (), s32[]{:S(2)}) async-start(), calls=%async_computation.4 | async-start | bytes 9437184 | tf_op jit(solution)/shard_map/reduce_scatter | solution.py:27
Sparse Core Ops, SparseCore 0:
  39.7 22.3 reduce-scatter.8
  65.1 22.4 reduce-scatter.6
  91.5 62.0 reduce-scatter.10
  156.8 69.0 all-reduce.2
  229.3 148.3 reduce-scatter.4
